TPU v7x, 32 devices: a whole 2x2x4 slice. The times are simulated.
32 devices in a mesh: px: 16 (over z, x, core), py: 2 (over y).
Axes of the slice: x: 2, y: 2, z: 4, core: 2. Of those that a mesh axis runs over, the one named last changes fastest.
Arguments:
- velocity: float32 [3, 1024, 2, 1024], P(None, 'px', 'py'), may hold values from -1.5 to 2.5
- band_of: int32 [2], replicated, may hold values from 0 to 1, as said below
Outputs:
- correlation: float32 [6, 2, 1024, 1024], P(None, None, ('px', 'py'))
Inputs may be any that keep to these rules, and one draw needn't show every extreme that they name: `band_of`: every band 0 to 1 holds at least one plane.
All inputs are finite; a program needn't handle non-finite values.
Results may differ from a plain program's by a relative error of at most 0.00013.
Values sent between devices are 32-bit elements; how exact they have to be, the bound alone decides.
A program may use at most 64 MiB of HBM per device.

v0:
```python
import math

import jax
import jax.numpy as jnp
from jax import lax
from jax.sharding import PartitionSpec as P

NB = 2


PAIR_LIST = ((0, 0), (0, 1), (0, 2), (1, 1), (1, 2), (2, 2))


def phase_table(row_values, offset, count, length):
    col_values = offset + lax.iota(jnp.int32, count)
    phase = row_values[:, None] * col_values[None, :] % length
    angle = phase.astype(jnp.float32) * (2.0 * math.pi / length)
    return (jnp.cos(angle), jnp.sin(angle))


def transform_last(real_part, imag_part, sign):
    full_shape = real_part.shape
    length = full_shape[-1]
    stacked = jnp.concatenate((real_part.reshape(-1, length), imag_part.reshape(-1, length)), 0)
    row_count = stacked.shape[0] // 2
    row_values = lax.iota(jnp.int32, length)

    def one_block(block_index, outputs):
        offset = (block_index * 128).astype(jnp.int32)
        cosine_table, sine_table = phase_table(row_values, offset, 128, length)
        with_cos = jnp.dot(
            stacked,
            cosine_table,
            precision=lax.Precision.HIGHEST,
            preferred_element_type=jnp.float32,
        )
        with_sin = jnp.dot(
            stacked, sine_table, precision=lax.Precision.HIGHEST, preferred_element_type=jnp.float32
        )
        new_real = with_cos[:row_count] - sign * with_sin[row_count:]
        new_imag = with_cos[row_count:] + sign * with_sin[:row_count]
        return (
            lax.dynamic_update_slice_in_dim(outputs[0], new_real, offset, 1),
            lax.dynamic_update_slice_in_dim(outputs[1], new_imag, offset, 1),
        )

    zeros = jnp.zeros((row_count, length), jnp.float32)
    out_real, out_imag = lax.fori_loop(0, length // 128, one_block, (zeros, zeros))
    return (out_real.reshape(full_shape), out_imag.reshape(full_shape))


def span_forward(velocity):
    comps, rows_x, planes, length = velocity.shape
    half = length // 2
    row_values = lax.iota(jnp.int32, length)

    def one_block(block_index, outputs):
        offset = (block_index * 128).astype(jnp.int32)
        cosine_table, sine_table = phase_table(row_values, offset, 128, length)
        with_cos = jnp.einsum(
            "cxpz,zk->cpkx",
            velocity,
            cosine_table,
            precision=lax.Precision.HIGHEST,
            preferred_element_type=jnp.float32,
        )
        with_sin = jnp.einsum(
            "cxpz,zk->cpkx",
            velocity,
            sine_table,
            precision=lax.Precision.HIGHEST,
            preferred_element_type=jnp.float32,
        )
        return (
            lax.dynamic_update_slice_in_dim(outputs[0], with_cos, offset, 2),
            lax.dynamic_update_slice_in_dim(outputs[1], -with_sin, offset, 2),
        )

    zeros = jnp.zeros((comps, planes, half, rows_x), jnp.float32)
    return lax.fori_loop(0, half // 128, one_block, (zeros, zeros))


def span_inverse(summed, kz_order):
    half = summed.shape[3]
    length = 2 * half
    multiplier = jnp.where(kz_order == 0, 1.0, 2.0).astype(jnp.float32)
    held_real = summed[:, :, 0] * multiplier[:, None]
    held_imag = summed[:, :, 1] * multiplier[:, None]

    def one_block(block_index, output):
        offset = (block_index * 128).astype(jnp.int32)
        cosine_table, sine_table = phase_table(kz_order, offset, 128, length)
        part = jnp.einsum(
            "sbkd,kz->sbdz",
            held_real,
            cosine_table,
            precision=lax.Precision.HIGHEST,
            preferred_element_type=jnp.float32,
        )
        part = part - jnp.einsum(
            "sbkd,kz->sbdz",
            held_imag,
            sine_table,
            precision=lax.Precision.HIGHEST,
            preferred_element_type=jnp.float32,
        )
        return lax.dynamic_update_slice_in_dim(output, part, offset, 3)

    zeros = jnp.zeros((summed.shape[0], summed.shape[1], summed.shape[4], length), jnp.float32)
    return lax.fori_loop(0, length // 128, one_block, zeros)


def per_device(velocity, band_of):
    px_count = lax.axis_size("px")
    py_count = lax.axis_size("py")
    comps, rows_x, planes, span = velocity.shape
    stream = rows_x * px_count
    half = span // 2
    local_k = half // px_count
    span_real, span_imag = span_forward(velocity)
    planes_spec = jnp.stack((span_real, span_imag), 1)
    kz_index = lax.iota(jnp.int32, local_k)
    kx_index = lax.iota(jnp.int32, stream)
    at_anchor = jnp.logical_and(
        lax.axis_index("px") == 0, jnp.logical_and(kz_index[:, None] == 0, kx_index[None, :] == 0)
    )
    keep_mask = 1.0 - at_anchor.astype(jnp.float32)
    received = lax.all_to_all(planes_spec, "px", split_axis=3, concat_axis=4, tiled=True)
    front_real, front_imag = transform_last(received[:, 0], received[:, 1], -1.0)
    spectrum = jnp.stack((front_real * keep_mask, front_imag * keep_mask), 1)
    cross_list = []
    for left_comp, right_comp in PAIR_LIST:
        left_real, left_imag = (spectrum[left_comp, 0], spectrum[left_comp, 1])
        right_real, right_imag = (spectrum[right_comp, 0], spectrum[right_comp, 1])
        cross_list.append(
            jnp.stack(
                (
                    left_real * right_real + left_imag * right_imag,
                    left_real * right_imag - left_imag * right_real,
                ),
                0,
            )
        )
    cross = jnp.stack(cross_list, 0)
    band_ids = lax.iota(jnp.int32, NB)
    onehot_all = (band_of[:, None] == band_ids[None, :]).astype(jnp.float32)
    counts = jnp.sum(onehot_all, 0)
    cells = float(stream * span)
    plane_start = lax.axis_index("py") * planes
    local_hot = lax.dynamic_slice_in_dim(onehot_all, plane_start, planes, 0)
    band_weight = local_hot / (counts[None, :] * (cells * math.sqrt(cells)))
    banded = jnp.einsum("sapkx,pb->sbakx", cross, band_weight, precision=lax.Precision.HIGHEST)
    summed = lax.psum_scatter(banded, "py", scatter_dimension=3, tiled=True)
    back_real, back_imag = transform_last(summed[:, :, 0], summed[:, :, 1], 1.0)
    exchanged = lax.all_to_all(
        lax.all_to_all(
            jnp.stack((back_real, back_imag), 2), "px", split_axis=4, concat_axis=3, tiled=True
        ),
        "py",
        split_axis=4,
        concat_axis=3,
        tiled=True,
    )
    quarter = local_k // py_count
    position = lax.iota(jnp.int32, half)
    outer = position // (px_count * quarter)
    remain = position % (px_count * quarter)
    kz_order = remain // quarter * local_k + outer * quarter + remain % quarter
    return span_inverse(exchanged, kz_order)


def solution(mesh):
    in_specs = (P(None, "px", "py", None), P())
    out_specs = P(None, None, ("px", "py"), None)
    return jax.shard_map(
        per_device, mesh=mesh, in_specs=in_specs, out_specs=out_specs, check_vma=False
    )
```

profile of v0, /device:TPU:0, one launch (start us, length us, event | category | flops | bytes accessed | tf_op | source)
XLA Modules:
  0.0 426.2 jit_solution(16905591505714499347)
XLA Ops:
  7.9 21.8 %while.70 = (s32[]{:T(128)}, f32[3,1,512,64]{2,3,0,1:T(8,128)S(1)}, f32[3,1,512,64]{2,3,0,1:T(8,128)S(1)}, f32[3,64,1,1024]{3,1,0,2:T(8,128)S(1)}, s32[]{:T(128)}, /*index=5*/s32[]{:T(128)}, s32[]{:T(128)}, s32[]{:T(128)}) while((s32[]{:T(128)}, f32[3,1,512,64]{2,3,0,1:T(8,128)S(1)}, f32[3,1,512,64]{2,3,0,1:T(8,128)S(1)}, ...), condition=%wide.region_2.3_spmd.clone, body=%wide.region_1.2_spmd.clone.sunk | while | flops 607674496 | bytes 1771151 | solution.py:80
  7.9 2.7 fusion.166
  10.6 2.7 fusion.165
  13.4 2.7 fusion.166
  16.1 2.7 fusion.165
  18.8 2.7 fusion.166
  21.5 2.7 fusion.165
  24.3 2.7 fusion.166
  27.0 2.7 fusion.165
  30.9 2.5 reshape.312
  33.5 7.4 %all-to-all-start = ((f32[16,1,12288]{2,1,0:T(1,128)}), f32[16,1,12288]{2,1,0:T(1,128)S(1)}, u32[]{:S(2)}, u32[]{:S(2)}) async-start(f32[16,1,12288]{2,1,0:T(1,128)} %reshape.312), calls=%async_computation | async-start | bytes 1572864 | tf_op jit(solution)/shard_map/all_to_all | solution.py:128
  41.4 18.1 %all-to-all-done = f32[16,1,12288]{2,1,0:T(1,128)S(1)} async-done(((f32[16,1,12288]{2,1,0:T(1,128)}), f32[16,1,12288]{2,1,0:T(1,128)S(1)}, u32[]{:S(2)}, u32[]{:S(2)}) %all-to-all-start) | async-done | bytes 786464 | tf_op jit(solution)/shard_map/all_to_all | solution.py:128
  60.0 2.4 reduce
  65.2 43.7 %while.71 = (s32[]{:T(128)}, f32[96,1024]{1,0:T(8,128)S(1)}, f32[96,1024]{1,0:T(8,128)S(1)}, f32[192,1024]{1,0:T(8,128)S(1)}, s32[]{:T(128)}, /*index=5*/s32[]{:T(128)}, s32[]{:T(128)}, s32[]{:T(128)}) while((s32[]{:T(128)}, f32[96,1024]{1,0:T(8,128)S(1)}, f32[96,1024]{1,0:T(8,128)S(1)}, f32[192,1024]{1,0:T(8,128)S(1)}, s32[]{:T(128)}, ...), condition=%wide.region_4.5_spmd.clone, body=%wide.region_3.4_spmd.clone.sunk | while | flops 607699072 | bytes 2066059 | solution.py:48
  65.3 2.7 convolution_bitcast_fusion.10
  68.0 2.7 convolution_bitcast_fusion.9
  70.7 2.7 convolution_bitcast_fusion.10
  73.4 2.7 convolution_bitcast_fusion.9
  76.2 2.7 convolution_bitcast_fusion.10
  78.9 2.7 convolution_bitcast_fusion.9
  81.6 2.7 convolution_bitcast_fusion.10
  84.3 2.7 convolution_bitcast_fusion.9
  87.1 2.7 convolution_bitcast_fusion.10
  89.8 2.7 convolution_bitcast_fusion.9
  92.6 2.7 convolution_bitcast_fusion.10
  95.2 2.7 convolution_bitcast_fusion.9
  98.0 2.7 convolution_bitcast_fusion.10
  100.7 2.7 convolution_bitcast_fusion.9
  103.5 2.7 convolution_bitcast_fusion.10
  106.2 2.7 convolution_bitcast_fusion.9
  109.4 2.1 multiply_bitcast_fusion
  111.5 44.3 %reduce-scatter.2.cloned.1.call-done = f32[6,2,2,16,1024]{4,3,1,0,2:T(8,128)} async-done(((f32[6,2,2,32,1024]{4,3,1,0,2:T(8,128)}), f32[6,2,2,16,1024]{4,3,1,0,2:T(8,128)}) %reduce-scatter.2.cloned.1.call-update) | async-done | bytes 1572880 | tf_op jit(solution)/shard_map/reduce_scatter | solution.py:153
  158.8 86.7 %while.72 = (s32[]{:T(128)}, f32[192,1024]{1,0:T(8,128)S(1)}, f32[192,1024]{1,0:T(8,128)S(1)}, f32[384,1024]{1,0:T(8,128)}, s32[]{:T(128)}, /*index=5*/s32[]{:T(128)}, s32[]{:T(128)}, s32[]{:T(128)}) while((s32[]{:T(128)}, f32[192,1024]{1,0:T(8,128)S(1)}, f32[192,1024]{1,0:T(8,128)S(1)}, f32[384,1024]{1,0:T(8,128)}, s32[]{:T(128)}, ...), condition=%wide.region_7.8_spmd.clone, body=%wide.region_6.7_spmd.clone.sunk | while | flops 1211678848 | bytes 4916875 | solution.py:48
  159.1 5.2 %convolution_bitcast_fusion.11 = f32[384,128]{0,1:T(8,128)S(1)} fusion(f32[384,1024]{1,0:T(8,128)} %get-tuple-element.844, s32[128]{0:T(128)S(1)} %iota_add_fusion.10), kind=kOutput, calls=%fused_computation.63.clone.1 | convolution fusion | flops 605814784 | bytes 1769984 | tf_op jit(solution)/shard_map/while/body/eval_jaxpr/dot_general | solution.py:37
  164.3 5.2 %convolution_bitcast_fusion.12 = f32[384,128]{0,1:T(8,128)S(1)} fusion(f32[384,1024]{1,0:T(8,128)} %get-tuple-element.844, s32[128]{0:T(128)S(1)} %iota_add_fusion.10), kind=kOutput, calls=%fused_computation.64.clone.1 | convolution fusion | flops 605814784 | bytes 1769984 | tf_op jit(solution)/shard_map/while/body/eval_jaxpr/dot_general | solution.py:31
  169.9 5.2 %convolution_bitcast_fusion.11 = f32[384,128]{0,1:T(8,128)S(1)} fusion(f32[384,1024]{1,0:T(8,128)} %get-tuple-element.844, s32[128]{0:T(128)S(1)} %iota_add_fusion.10), kind=kOutput, calls=%fused_computation.63.clone.1 | convolution fusion | flops 605814784 | bytes 1769984 | tf_op jit(solution)/shard_map/while/body/eval_jaxpr/dot_general | solution.py:37
  175.1 5.2 %convolution_bitcast_fusion.12 = f32[384,128]{0,1:T(8,128)S(1)} fusion(f32[384,1024]{1,0:T(8,128)} %get-tuple-element.844, s32[128]{0:T(128)S(1)} %iota_add_fusion.10), kind=kOutput, calls=%fused_computation.64.clone.1 | convolution fusion | flops 605814784 | bytes 1769984 | tf_op jit(solution)/shard_map/while/body/eval_jaxpr/dot_general | solution.py:31
  180.7 5.2 %convolution_bitcast_fusion.11 = f32[384,128]{0,1:T(8,128)S(1)} fusion(f32[384,1024]{1,0:T(8,128)} %get-tuple-element.844, s32[128]{0:T(128)S(1)} %iota_add_fusion.10), kind=kOutput, calls=%fused_computation.63.clone.1 | convolution fusion | flops 605814784 | bytes 1769984 | tf_op jit(solution)/shard_map/while/body/eval_jaxpr/dot_general | solution.py:37
  185.9 5.2 %convolution_bitcast_fusion.12 = f32[384,128]{0,1:T(8,128)S(1)} fusion(f32[384,1024]{1,0:T(8,128)} %get-tuple-element.844, s32[128]{0:T(128)S(1)} %iota_add_fusion.10), kind=kOutput, calls=%fused_computation.64.clone.1 | convolution fusion | flops 605814784 | bytes 1769984 | tf_op jit(solution)/shard_map/while/body/eval_jaxpr/dot_general | solution.py:31
  191.5 5.2 %convolution_bitcast_fusion.11 = f32[384,128]{0,1:T(8,128)S(1)} fusion(f32[384,1024]{1,0:T(8,128)} %get-tuple-element.844, s32[128]{0:T(128)S(1)} %iota_add_fusion.10), kind=kOutput, calls=%fused_computation.63.clone.1 | convolution fusion | flops 605814784 | bytes 1769984 | tf_op jit(solution)/shard_map/while/body/eval_jaxpr/dot_general | solution.py:37
  196.7 5.2 %convolution_bitcast_fusion.12 = f32[384,128]{0,1:T(8,128)S(1)} fusion(f32[384,1024]{1,0:T(8,128)} %get-tuple-element.844, s32[128]{0:T(128)S(1)} %iota_add_fusion.10), kind=kOutput, calls=%fused_computation.64.clone.1 | convolution fusion | flops 605814784 | bytes 1769984 | tf_op jit(solution)/shard_map/while/body/eval_jaxpr/dot_general | solution.py:31
  202.3 5.2 %convolution_bitcast_fusion.11 = f32[384,128]{0,1:T(8,128)S(1)} fusion(f32[384,1024]{1,0:T(8,128)} %get-tuple-element.844, s32[128]{0:T(128)S(1)} %iota_add_fusion.10), kind=kOutput, calls=%fused_computation.63.clone.1 | convolution fusion | flops 605814784 | bytes 1769984 | tf_op jit(solution)/shard_map/while/body/eval_jaxpr/dot_general | solution.py:37
  207.5 5.2 %convolution_bitcast_fusion.12 = f32[384,128]{0,1:T(8,128)S(1)} fusion(f32[384,1024]{1,0:T(8,128)} %get-tuple-element.844, s32[128]{0:T(128)S(1)} %iota_add_fusion.10), kind=kOutput, calls=%fused_computation.64.clone.1 | convolution fusion | flops 605814784 | bytes 1769984 | tf_op jit(solution)/shard_map/while/body/eval_jaxpr/dot_general | solution.py:31
  213.1 5.2 %convolution_bitcast_fusion.11 = f32[384,128]{0,1:T(8,128)S(1)} fusion(f32[384,1024]{1,0:T(8,128)} %get-tuple-element.844, s32[128]{0:T(128)S(1)} %iota_add_fusion.10), kind=kOutput, calls=%fused_computation.63.clone.1 | convolution fusion | flops 605814784 | bytes 1769984 | tf_op jit(solution)/shard_map/while/body/eval_jaxpr/dot_general | solution.py:37
  218.3 5.2 %convolution_bitcast_fusion.12 = f32[384,128]{0,1:T(8,128)S(1)} fusion(f32[384,1024]{1,0:T(8,128)} %get-tuple-element.844, s32[128]{0:T(128)S(1)} %iota_add_fusion.10), kind=kOutput, calls=%fused_computation.64.clone.1 | convolution fusion | flops 605814784 | bytes 1769984 | tf_op jit(solution)/shard_map/while/body/eval_jaxpr/dot_general | solution.py:31
  223.9 5.2 %convolution_bitcast_fusion.11 = f32[384,128]{0,1:T(8,128)S(1)} fusion(f32[384,1024]{1,0:T(8,128)} %get-tuple-element.844, s32[128]{0:T(128)S(1)} %iota_add_fusion.10), kind=kOutput, calls=%fused_computation.63.clone.1 | convolution fusion | flops 605814784 | bytes 1769984 | tf_op jit(solution)/shard_map/while/body/eval_jaxpr/dot_general | solution.py:37
  229.1 5.2 %convolution_bitcast_fusion.12 = f32[384,128]{0,1:T(8,128)S(1)} fusion(f32[384,1024]{1,0:T(8,128)} %get-tuple-element.844, s32[128]{0:T(128)S(1)} %iota_add_fusion.10), kind=kOutput, calls=%fused_computation.64.clone.1 | convolution fusion | flops 605814784 | bytes 1769984 | tf_op jit(solution)/shard_map/while/body/eval_jaxpr/dot_general | solution.py:31
  234.7 5.2 %convolution_bitcast_fusion.11 = f32[384,128]{0,1:T(8,128)S(1)} fusion(f32[384,1024]{1,0:T(8,128)} %get-tuple-element.844, s32[128]{0:T(128)S(1)} %iota_add_fusion.10), kind=kOutput, calls=%fused_computation.63.clone.1 | convolution fusion | flops 605814784 | bytes 1769984 | tf_op jit(solution)/shard_map/while/body/eval_jaxpr/dot_general | solution.py:37
  239.9 5.2 %convolution_bitcast_fusion.12 = f32[384,128]{0,1:T(8,128)S(1)} fusion(f32[384,1024]{1,0:T(8,128)} %get-tuple-element.844, s32[128]{0:T(128)S(1)} %iota_add_fusion.10), kind=kOutput, calls=%fused_computation.64.clone.1 | convolution fusion | flops 605814784 | bytes 1769984 | tf_op jit(solution)/shard_map/while/body/eval_jaxpr/dot_general | solution.py:31
  245.7 13.2 %copy.46 = f32[6,2,2,16,1024]{3,1,0,2,4:T(2,128)} copy(f32[6,2,2,16,1024]{4,3,1,0,2:T(8,128)S(1)} %pad_maximum_fusion.1) | data formatting | bytes 3145728 | tf_op jit(solution)/shard_map/stack | solution.py:157
  258.9 18.6 %reshape.314 = f32[16,1,24576]{2,1,0:T(1,128)S(1)} reshape(f32[1024,2,6,2,16]{4,3,2,1,0:T(2,128)} %bitcast.165) | data formatting | bytes 3145728
  277.5 41.7 %all_to_all.54 = f32[16,1,24576]{2,1,0:T(1,128)S(1)} all-to-all(f32[16,1,24576]{2,1,0:T(1,128)S(1)} %reshape.314), channel_id=1, replica_groups=mesh['px'=16,'py'=2] {'px'}, dimensions={0} | all-to-all | bytes 3145728 | tf_op jit(solution)/shard_map/all_to_all | solution.py:156
  319.3 4.3 %reduce.1 = f32[16,24576]{1,0:T(8,128)S(1)} reduce(f32[16,1,24576]{2,1,0:T(1,128)S(1)} %all_to_all.54, f32[]{:T(128)} %broadcast.407), dimensions={1}, to_apply=%all_to_all.43.reduce_sub_computation | reduce | bytes 3145732 | tf_op jit(solution)/shard_map/all_to_all | solution.py:156
  323.6 22.1 %reshape.315 = f32[1024,2,6,2,16]{4,3,2,1,0:T(2,128)} reshape(f32[16,24576]{1,0:T(8,128)S(1)} %reduce.1) | data formatting | bytes 3145728
  345.8 15.4 %copy.47 = f32[6,2,2,16,16,64]{5,3,4,2,1,0:T(8,128)S(1)} copy(f32[6,2,2,16,16,64]{3,1,0,2,5,4:T(2,128)} %bitcast.166) | data formatting | bytes 3145728 | tf_op jit(solution)/shard_map/all_to_all | solution.py:156
  361.1 2.4 copy.48
  363.5 3.7 all-to-all-start.2
  367.2 20.6 %all-to-all-done.2 = f32[6,2,2,256,64]{3,2,1,0,4:T(2,128)S(1)} async-done(((f32[6,2,2,256,64]{3,2,1,0,4:T(2,128)}), f32[6,2,2,256,64]{3,2,1,0,4:T(2,128)S(1)}, u32[]{:S(2)}, u32[]{:S(2)}) %all-to-all-start.2) | async-done | bytes 1572896 | tf_op jit(solution)/shard_map/all_to_all | solution.py:155
  389.0 29.0 %while.73 = (s32[]{:T(128)}, f32[6,2,32,1024]{3,2,1,0:T(8,128)S(1)}, f32[6,2,512,32]{2,3,1,0:T(8,128)S(1)}, f32[6,2,512,32]{2,3,1,0:T(8,128)S(1)}, s32[]{:T(128)}, /*index=5*/s32[]{:T(128)}, s32[]{:T(128)}, s32[]{:T(128)}) while((s32[]{:T(128)}, f32[6,2,32,1024]{3,2,1,0:T(8,128)S(1)}, f32[6,2,512,32]{2,3,1,0:T(8,128)S(1)}, ...), condition=%wide.region_9.10_spmd.clone, body=%wide.region_8.9_spmd.clone.sunk | while | flops 605881984 | bytes 2170507 | solution.py:110
  391.0 1.8 fusion.182
  394.6 1.8 fusion.182
  398.2 1.8 fusion.182
  405.4 1.8 fusion.182
  412.6 1.8 fusion.182
  (132 shorter events, 34.5 us)
Async XLA Ops:
  30.9 10.2 %copy-start.1 = (s32[2]{0:T(128)S(1)}, s32[2]{0:T(128)}, u32[]{:S(2)}) copy-start(s32[2]{0:T(128)} %param.11) | copy-start | bytes 28
  33.5 26.1 %all-to-all-start = ((f32[16,1,12288]{2,1,0:T(1,128)}), f32[16,1,12288]{2,1,0:T(1,128)S(1)}, u32[]{:S(2)}, u32[]{:S(2)}) async-start(f32[16,1,12288]{2,1,0:T(1,128)} %reshape.312), calls=%async_computation | async-start | bytes 1572864 | tf_op jit(solution)/shard_map/all_to_all | solution.py:128
  40.8 115.0 %reduce-scatter.2.cloned.1.call-start = ((), (), s32[]{:S(2)}) async-start(), calls=%async_computation.4 | async-start | bytes 4718592 | tf_op jit(solution)/shard_map/reduce_scatter | solution.py:153
  363.5 24.3 %all-to-all-start.2 = ((f32[6,2,2,256,64]{3,2,1,0,4:T(2,128)}), f32[6,2,2,256,64]{3,2,1,0,4:T(2,128)S(1)}, u32[]{:S(2)}, u32[]{:S(2)}) async-start(f32[6,2,2,256,64]{3,2,1,0,4:T(2,128)} %copy.48), calls=%async_computation.3 | async-start | bytes 3145728 | tf_op jit(solution)/shard_map/all_to_all | solution.py:155
  418.0 1.1 copy-start
Sparse Core Ops, SparseCore 0:
  111.6 44.1 reduce-scatter.1
where the time goes:
time: 433 us; the launch traced here: 426 us
  matrix products  176 us (41%)
  local copies, waits for them, and re-layouts  85.2 us (20%)
  waiting for transfers between devices  83.1 us (19%)
  blocking collectives  41.7 us (10%)
  between operations  13.9 us (3%)
  other arithmetic  12.7 us (3%)
  starting transfers between devices  11.3 us (3%)
    dot_general x16, matrix products, one_block(): jnp.dot(stacked, sine_table, precision=lax.Precision.HIGHEST, preferred_e...  63.3 us
    dot_general x16, matrix products, one_block(): jnp.dot(stacked, cosine_table, precision=lax.Precision.HIGHEST, preferred...  63 us
    unnamed x9, local copies, waits for them, and re-layouts  46.8 us
    reduce_scatter x1, waiting for transfers between devices, per_device(): summed = lax.psum_scatter(banded, 'py', scatter_dimension=3, tiled=True)  44.3 us
    all_to_all x1, blocking collectives, per_device(): lax.all_to_all(jnp.stack((back_real, back_imag), 2), 'px', split_axis=4,...  41.7 us
    all_to_all x1, waiting for transfers between devices, per_device(): lax.all_to_all(lax.all_to_all(jnp.stack((back_real, back_imag), 2), 'px',...  20.6 us
    all_to_all x1, waiting for transfers between devices, per_device(): lax.all_to_all(planes_spec, 'px', split_axis=3, concat_axis=4, tiled=True)  18.1 us
    all_to_all x2, local copies, waits for them, and re-layouts, per_device(): lax.all_to_all(jnp.stack((back_real, back_imag), 2), 'px', split_axis=4,...  17.8 us
  transfers between devices with their start and end apart: 3, of which 3 were waited for; matrix products, arithmetic and copies ran while one was open for 0% of the time, Pallas kernels for 0%

commit v1 on v0

--- a/solution.py
+++ b/solution.py
@@ -1,8 +1,12 @@
+import functools
 import math
 
 import jax
 import jax.numpy as jnp
+import numpy as np
 from jax import lax
+from jax.experimental import pallas as pl
+from jax.experimental.pallas import tpu as pltpu
 from jax.sharding import PartitionSpec as P
 
 NB = 2
@@ -110,7 +114,7 @@
     return lax.fori_loop(0, length // 128, one_block, zeros)
 
 
-def per_device(velocity, band_of):
+def general_device(velocity, band_of):
     px_count = lax.axis_size("px")
     py_count = lax.axis_size("py")
     comps, rows_x, planes, span = velocity.shape
@@ -169,6 +173,374 @@
     return span_inverse(exchanged, kz_order)
 
 
+def split_table(table):
+    high = table.astype(jnp.bfloat16)
+    low = (table - high.astype(np.float64)).astype(jnp.bfloat16)
+    return high, low
+
+
+def span_tables(length):
+    quarter, eighth = length // 4, length // 8
+    column = np.arange(quarter)
+
+    def angle(first, count):
+        wave = 4 * np.arange(count) + first
+        return 2.0 * np.pi * ((wave[:, None] * column[None, :]) % length) / length
+
+    even = angle(0, eighth)
+    middle = angle(2, eighth)
+    odd = angle(1, quarter)
+    table_even = np.concatenate((np.cos(even), -np.sin(even)), 0)
+    table_middle = np.concatenate((np.cos(middle), -np.sin(middle)), 0)
+    table_odd = np.block([[np.cos(odd), -np.sin(odd)], [-np.sin(odd), -np.cos(odd)]])
+    return split_table(table_even) + split_table(table_middle) + split_table(table_odd)
+
+
+def stream_tables(length):
+    quarter = length // 4
+    index = np.arange(quarter)
+    angle = 2.0 * np.pi * ((index[:, None] * index[None, :]) % quarter) / quarter
+    cosine, sine = np.cos(angle), np.sin(angle)
+    twist = 2.0 * np.pi * (np.arange(4)[:, None] * index[None, :]) / length
+    twiddle = np.concatenate((np.cos(twist), np.sin(twist)), 0).astype(np.float32)
+    return split_table(np.block([[cosine, -sine], [sine, cosine]])) + (twiddle,)
+
+
+def split_value(value):
+    high = value.astype(jnp.bfloat16)
+    low = (value - high.astype(jnp.float32)).astype(jnp.bfloat16)
+    return high, low
+
+
+def three_dots(left, right, dims):
+    def one(a, b):
+        return lax.dot_general(a, b, (dims, ((), ())), preferred_element_type=jnp.float32)
+
+    return one(left[0], right[0]) + (one(left[1], right[0]) + one(left[0], right[1]))
+
+
+NT = ((1,), (1,))
+NN = ((1,), (0,))
+
+
+def span_kernel(share, v_ref, e_h, e_l, m_h, m_l, o_h, o_l, out_ref):
+    values = v_ref[...]
+    rows = values.shape[0] // 3
+    values = jnp.concatenate((values, values[2 * rows :]), 0)
+    quarter = values.shape[1] // 4
+    part = [values[:, i * quarter : (i + 1) * quarter] for i in range(4)]
+    plus_even, plus_odd = part[0] + part[2], part[1] + part[3]
+    odd_in = jnp.concatenate((part[0] - part[2], part[1] - part[3]), 1)
+    even = three_dots((e_h[...], e_l[...]), split_value(plus_even + plus_odd), NT)
+    middle = three_dots((m_h[...], m_l[...]), split_value(plus_even - plus_odd), NT)
+    odd = three_dots((o_h[...], o_l[...]), split_value(odd_in), NT)
+    eighth = quarter // 2
+    real = jnp.concatenate((even[:eighth], middle[:eighth], odd[:quarter]), 0)
+    imag = jnp.concatenate((even[eighth:], middle[eighth:], odd[quarter:]), 0)
+    lane = lax.broadcasted_iota(jnp.int32, (real.shape[0], 128), 1)
+    third = jnp.where(lane < 64, real[:, 128:], imag[:, 128:])
+    out_ref[:, :share] = real[:, :128].reshape(-1, share, 128)
+    out_ref[:, share : 2 * share] = imag[:, :128].reshape(-1, share, 128)
+    out_ref[:, 2 * share :] = third.reshape(-1, share, 128)
+
+
+def stream_kernel(share, planes, me_ref, weight_ref, in_ref, t_h, t_l, w_ref, out_ref):
+    first_device = me_ref[0] == 0
+    px_count = in_ref.shape[0] // planes
+    columns = px_count // 2
+    group_cols = columns // 4
+    quarter = w_ref.shape[1]
+    lane = lax.broadcasted_iota(jnp.int32, (3 * share, 128), 1)
+    low_half = lane < 64
+    cells = []
+    for q in range(columns):
+        real, imag = [[], [], []], [[], [], []]
+        for y in range(planes):
+            a = in_ref[2 * q * planes + y]
+            b = in_ref[(2 * q + 1) * planes + y]
+            low = jnp.where(low_half, a, pltpu.roll(b, 64, 1))
+            high = jnp.where(low_half, pltpu.roll(a, 64, 1), b)
+            real[0].append(low[:share])
+            imag[0].append(low[share : 2 * share])
+            real[1].append(high[:share])
+            imag[1].append(high[share : 2 * share])
+            real[2].append(low[2 * share :])
+            imag[2].append(high[2 * share :])
+        cells.append(
+            (
+                jnp.concatenate(real[0] + real[1] + real[2], 0),
+                jnp.concatenate(imag[0] + imag[1] + imag[2], 0),
+            )
+        )
+    part = [
+        tuple(
+            jnp.concatenate([cells[j * group_cols + g][ri] for g in range(group_cols)], 1)
+            for ri in range(2)
+        )
+        for j in range(4)
+    ]
+    sum02 = [part[0][i] + part[2][i] for i in range(2)]
+    dif02 = [part[0][i] - part[2][i] for i in range(2)]
+    sum13 = [part[1][i] + part[3][i] for i in range(2)]
+    dif13 = [part[1][i] - part[3][i] for i in range(2)]
+    mixed = [
+        (sum02[0] + sum13[0], sum02[1] + sum13[1]),
+        (dif02[0] + dif13[1], dif02[1] - dif13[0]),
+        (sum02[0] - sum13[0], sum02[1] - sum13[1]),
+        (dif02[0] - dif13[1], dif02[1] + dif13[0]),
+    ]
+    turned = []
+    for k1, (real, imag) in enumerate(mixed):
+        if k1:
+            cosine, sine = w_ref[k1 : k1 + 1], w_ref[4 + k1 : 5 + k1]
+            real, imag = real * cosine + imag * sine, imag * cosine - real * sine
+        turned.append(jnp.concatenate((real, imag), 1))
+    table = (t_h[...], t_l[...])
+    front = three_dots(split_value(jnp.concatenate(turned, 0)), table, NN)
+    block = 3 * planes * share
+    row = lax.broadcasted_iota(jnp.int32, (block, 2 * quarter), 0)
+    col = lax.broadcasted_iota(jnp.int32, (block, 2 * quarter), 1)
+    anchor = jnp.logical_and(row % share == 0, col % quarter == 0)
+    anchor = jnp.logical_and(anchor, first_device)
+    front = jnp.concatenate((jnp.where(anchor, 0.0, front[:block]), front[block:]), 0)
+    front = front.reshape(4, 3, planes, share, 2 * quarter)
+    field = [
+        [
+            (
+                front[:, c, y, :, :quarter].reshape(4 * share, quarter),
+                front[:, c, y, :, quarter:].reshape(4 * share, quarter),
+            )
+            for y in range(planes)
+        ]
+        for c in range(3)
+    ]
+    row = lax.broadcasted_iota(jnp.int32, (4 * share, quarter), 0)
+    single = jnp.logical_and(row % share == 0, first_device)
+    multiplier = jnp.where(single, 1.0, 2.0)
+    own, mutual = [], []
+    for left, right in PAIR_LIST:
+        real_sum, imag_sum = [None] * NB, [None] * NB
+        for y in range(planes):
+            lr, li = field[left][y]
+            rr, ri = field[right][y]
+            real = lr * rr + li * ri
+            imag = None if left == right else lr * ri - li * rr
+            for b in range(NB):
+                weight = weight_ref[y * NB + b]
+                add = weight * real
+                real_sum[b] = add if y == 0 else real_sum[b] + add
+                if imag is not None:
+                    add = weight * imag
+                    imag_sum[b] = add if y == 0 else imag_sum[b] + add
+        for b in range(NB):
+            if left == right:
+                own.append(real_sum[b] * multiplier)
+            else:
+                mutual.append(
+                    jnp.concatenate((real_sum[b] * multiplier, imag_sum[b] * multiplier), 1)
+                )
+    own_table = (t_h[:, :quarter], t_l[:, :quarter])
+    own_back = three_dots(split_value(jnp.concatenate(own, 0)), own_table, NT)
+    mutual_back = three_dots(split_value(jnp.concatenate(mutual, 0)), table, NT)
+    lines = []
+    own_at = mutual_at = 0
+    for left, right in PAIR_LIST:
+        for b in range(NB):
+            if left == right:
+                back = own_back[own_at * 4 * share : (own_at + 1) * 4 * share]
+                own_at += 1
+            else:
+                back = mutual_back[mutual_at * 4 * share : (mutual_at + 1) * 4 * share]
+                mutual_at += 1
+            turned = []
+            for k1 in range(4):
+                real = back[k1 * share : (k1 + 1) * share, :quarter]
+                imag = back[k1 * share : (k1 + 1) * share, quarter:]
+                if k1:
+                    cosine, sine = w_ref[k1 : k1 + 1], w_ref[4 + k1 : 5 + k1]
+                    real, imag = real * cosine - imag * sine, imag * cosine + real * sine
+                turned.append((real, imag))
+            s02 = [turned[0][i] + turned[2][i] for i in range(2)]
+            d02 = [turned[0][i] - turned[2][i] for i in range(2)]
+            s13 = [turned[1][i] + turned[3][i] for i in range(2)]
+            d13 = [turned[1][i] - turned[3][i] for i in range(2)]
+            real = (s02[0] + s13[0], d02[0] - d13[1], s02[0] - s13[0], d02[0] + d13[1])
+            imag = (s02[1] + s13[1], d02[1] + d13[0], s02[1] - s13[1], d02[1] - d13[0])
+            lines.append((real, imag))
+    width = 4 * quarter // in_ref.shape[0]
+    groups = 128 // width
+    per_group = len(lines) // groups
+    lane = lax.broadcasted_iota(jnp.int32, (share, 128), 1)
+    for i in range(per_group):
+        for ri in range(2):
+            at = (2 * i + ri) * share
+            for q in range(4 * quarter // 128):
+                j, inside = q * 128 // quarter, q * 128 % quarter
+                tiles = [
+                    lines[g * per_group + i][ri][j][:, inside : inside + 128]
+                    for g in range(groups)
+                ]
+                for t in range(groups):
+                    packed = None
+                    for g in range(groups):
+                        shift = (g - t) * width % 128
+                        tile = pltpu.roll(tiles[g], shift, 1) if shift else tiles[g]
+                        packed = tile if g == 0 else jnp.where(lane >= g * width, tile, packed)
+                    out_ref[q * groups + t, at : at + share] = packed
+
+
+def back_kernel(share, in_ref, e_h, e_l, m_h, m_l, o_h, o_l, out_ref):
+    devices = in_ref.shape[0]
+    groups, per_group, width, length = out_ref.shape
+    quarter, eighth = length // 4, length // 8
+    for i in range(per_group):
+        at = 2 * i * share
+        real = in_ref[:, at : at + share].reshape(devices * share, 128).T
+        imag = in_ref[:, at + share : at + 2 * share].reshape(devices * share, 128).T
+
+        def both(start, stop):
+            return split_value(jnp.concatenate((real[:, start:stop], imag[:, start:stop]), 1))
+
+        even = three_dots(both(0, eighth), (e_h[...], e_l[...]), NN)
+        middle = three_dots(both(eighth, quarter), (m_h[...], m_l[...]), NN)
+        odd = three_dots(both(quarter, 2 * quarter), (o_h[...], o_l[...]), NN)
+        plus, minus = even + middle, even - middle
+        first, second = odd[:, :quarter], odd[:, quarter:]
+        for j, line in enumerate((plus + first, minus + second, plus - first, minus - second)):
+            out_ref[:, i, :, j * quarter : (j + 1) * quarter] = line.reshape(groups, width, quarter)
+
+
+def swap_kernel(px_count, py_count, in_ref, out_ref, send_sem, recv_sem, own_sem):
+    px, py = lax.axis_index("px"), lax.axis_index("py")
+    me = px * py_count + py
+    count = px_count * py_count
+    barrier = pltpu.get_barrier_semaphore()
+
+    def peer(step):
+        other_px = lax.rem(px + step // py_count, px_count)
+        other_py = lax.rem(py + step % py_count, py_count)
+        return other_px, other_py
+
+    for step in range(1, count):
+        pl.semaphore_signal(
+            barrier, inc=1, device_id=peer(step), device_id_type=pl.DeviceIdType.MESH
+        )
+    own = pltpu.make_async_copy(in_ref.at[me], out_ref.at[me], own_sem)
+    own.start()
+    pl.semaphore_wait(barrier, count - 1)
+    copies = []
+    order = sorted(range(1, count), key=lambda s: -min(s, count - s))
+    for step in order:
+        other = peer(step)
+        copy = pltpu.make_async_remote_copy(
+            src_ref=in_ref.at[other[0] * py_count + other[1]],
+            dst_ref=out_ref.at[me],
+            send_sem=send_sem.at[step],
+            recv_sem=recv_sem.at[step],
+            device_id=other,
+            device_id_type=pl.DeviceIdType.MESH,
+        )
+        copy.start()
+        copies.append(copy)
+    own.wait()
+    for copy in copies:
+        copy.wait()
+
+
+REMOTE = False
+
+
+def swap_blocks(value, px_count, py_count, collective):
+    if not REMOTE:
+        return lax.all_to_all(value, ("px", "py"), split_axis=0, concat_axis=0, tiled=True)
+    count = px_count * py_count
+    space = pl.BlockSpec(memory_space=pltpu.VMEM)
+    return pl.pallas_call(
+        functools.partial(swap_kernel, px_count, py_count),
+        out_shape=jax.ShapeDtypeStruct(value.shape, value.dtype),
+        in_specs=[space],
+        out_specs=space,
+        scratch_shapes=[
+            pltpu.SemaphoreType.DMA((count,)),
+            pltpu.SemaphoreType.DMA((count,)),
+            pltpu.SemaphoreType.DMA,
+        ],
+        compiler_params=pltpu.CompilerParams(collective_id=collective, has_side_effects=True),
+    )(value)
+
+
+def register_device(velocity, band_of):
+    px_count = lax.axis_size("px")
+    py_count = lax.axis_size("py")
+    count = px_count * py_count
+    _, rows_x, _, span = velocity.shape
+    stream = rows_x * px_count
+    share = span // 2 // count
+    width = stream // count
+    groups = 128 // width
+    per_group = len(PAIR_LIST) * NB // groups
+    vmem = pl.BlockSpec(memory_space=pltpu.VMEM)
+    smem = pl.BlockSpec(memory_space=pltpu.SMEM)
+    tables = span_tables(span)
+    params = pltpu.CompilerParams(vmem_limit_bytes=48 * 1024 * 1024)
+    spec = pl.pallas_call(
+        functools.partial(span_kernel, share),
+        out_shape=jax.ShapeDtypeStruct((count, 3 * share, 128), jnp.float32),
+        in_specs=[vmem] * 7,
+        out_specs=vmem,
+        compiler_params=params,
+    )(velocity.reshape(3 * rows_x, span), *tables)
+    spec = swap_blocks(spec, px_count, py_count, 0)
+    band_ids = lax.iota(jnp.int32, NB)
+    onehot = (band_of[:, None] == band_ids[None, :]).astype(jnp.float32)
+    cells = float(stream * span)
+    weight = onehot / (jnp.sum(onehot, 0)[None, :] * (cells * math.sqrt(cells)))
+    me = (lax.axis_index("px") * py_count + lax.axis_index("py")).astype(jnp.int32)
+    back = pl.pallas_call(
+        functools.partial(stream_kernel, share, py_count),
+        out_shape=jax.ShapeDtypeStruct((count, 2 * per_group * share, 128), jnp.float32),
+        in_specs=[smem, smem] + [vmem] * 4,
+        out_specs=vmem,
+        compiler_params=params,
+    )(me.reshape(1), weight.reshape(-1), spec, *stream_tables(stream))
+    back = swap_blocks(back, px_count, py_count, 1)
+    out = pl.pallas_call(
+        functools.partial(back_kernel, share),
+        out_shape=jax.ShapeDtypeStruct((groups, per_group, width, span), jnp.float32),
+        in_specs=[vmem] * 7,
+        out_specs=vmem,
+        compiler_params=params,
+    )(back, *tables)
+    return out.reshape(len(PAIR_LIST), NB, width, span)
+
+
+def fills_registers(velocity, px_count, py_count):
+    comps, rows_x, planes, span = velocity.shape
+    count = px_count * py_count
+    stream = rows_x * px_count
+    share = span // 2 // count
+    width = max(stream // count, 1)
+    return (
+        comps == 3
+        and rows_x == 64
+        and planes == 1
+        and px_count % 8 == 0
+        and span % 1024 == 0
+        and stream % 512 == 0
+        and stream == width * count
+        and span == 2 * share * count
+        and share % 8 == 0
+        and 128 % width == 0
+        and len(PAIR_LIST) * NB * width % 128 == 0
+    )
+
+
+def per_device(velocity, band_of):
+    if fills_registers(velocity, lax.axis_size("px"), lax.axis_size("py")):
+        return register_device(velocity, band_of)
+    return general_device(velocity, band_of)
+
+
 def solution(mesh):
     in_specs = (P(None, "px", "py", None), P())
     out_specs = P(None, None, ("px", "py"), None)

time: 433 us -> 78.6 us (0.18); the launches traced: 426 us -> 77.8 us
  matrix products: 176 us -> 0 us
  local copies, waits for them, and re-layouts: 85.2 us -> 1.64 us
  waiting for transfers between devices: 83.1 us -> 20.3 us
  between operations: 13.9 us -> 0.08 us
  other arithmetic: 12.7 us -> 0.16 us
  Pallas kernels: 0 us -> 7.36 us
    dot_general x56 -> x0, matrix products: 176 us -> none  [the longest x16 63.3 us: one_block(): jnp.dot(stacked, sine_table, precision=lax.Precision.HIGHEST, preferred_e...]
    unnamed x9 -> x21, local copies, waits for them, and re-layouts: 46.8 us -> 1.55 us
    reduce_scatter x1 -> x0, waiting for transfers between devices: 44.3 us -> none  [per_device(): summed = lax.psum_scatter(banded, 'py', scatter_dimension=3, tiled=True)]
    all_to_all x8 -> x0, local copies, waits for them, and re-layouts: 20.4 us -> none  [the longest x2 17.8 us: per_device(): lax.all_to_all(jnp.stack((back_real, back_imag), 2), 'px', split_axis=4,...]
    all_to_all x2 -> x1, waiting for transfers between devices: 38.7 us -> 20.3 us  [swap_blocks(): lax.all_to_all(value, ('px', 'py'), split_axis=0, concat_axis=0, tiled=True)]
    another operation x2 -> x0, local copies, waits for them, and re-layouts: 14.3 us -> none  [the longest x1 13.2 us: per_device(): jnp.stack((back_real, back_imag), 2)]
    pallas_call x0 -> x3, Pallas kernels: none -> 7.36 us  [the longest x1 3.33 us: register_device(): pl.pallas_call(functools.partial(stream_kernel, share, py_count), out_sha...]
    all_to_all x2 -> x0, other arithmetic: 6.73 us -> none  [the longest x1 4.32 us: per_device(): lax.all_to_all(jnp.stack((back_real, back_imag), 2), 'px', split_axis=4,...]
  transfers between devices with their start and end apart: 3 -> 1, of which waited for: 3 -> 1; matrix products, arithmetic and copies ran while one was open for 0% -> 0% of each run, Pallas kernels for 0% -> 0%
where the time goes in v1:
time: 78.6 us; the launch traced here: 77.8 us
  blocking collectives  40.9 us (52%)
  waiting for transfers between devices  20.3 us (26%)
  Pallas kernels  7.36 us (9%)
  starting transfers between devices  7.34 us (9%)
  local copies, waits for them, and re-layouts  1.64 us (2%)
    all_to_all x1, blocking collectives, swap_blocks(): lax.all_to_all(value, ('px', 'py'), split_axis=0, concat_axis=0, tiled=True)  40.9 us
    all_to_all x1, waiting for transfers between devices, swap_blocks(): lax.all_to_all(value, ('px', 'py'), split_axis=0, concat_axis=0, tiled=True)  20.3 us
    all_to_all x1, starting transfers between devices, swap_blocks(): lax.all_to_all(value, ('px', 'py'), split_axis=0, concat_axis=0, tiled=True)  7.34 us
    pallas_call x1, Pallas kernels, register_device(): pl.pallas_call(functools.partial(stream_kernel, share, py_count), out_sha...  3.33 us
    pallas_call x1, Pallas kernels, register_device(): pl.pallas_call(functools.partial(back_kernel, share), out_shape=jax.Shape...  2.32 us
    pallas_call x1, Pallas kernels, register_device(): pl.pallas_call(functools.partial(span_kernel, share), out_shape=jax.Shape...  1.71 us
  transfers between devices with their start and end apart: 1, of which 1 were waited for; matrix products, arithmetic and copies ran while one was open for 0% of the time, Pallas kernels for 0%

profile of v1, /device:TPU:0, one launch (start us, length us, event | category | flops | bytes accessed | tf_op | source)
XLA Modules:
  0.0 77.8 jit_solution(17462110050218928251)
XLA Ops:
  0.0 0.0 copy-start
  0.0 0.0 copy-start.1
  0.0 0.0 copy-start.4
  0.0 0.0 copy-start.5
  0.0 0.0 copy-start.6
  0.0 0.0 copy-start.7
  0.0 1.4 %copy.12 = f32[3,64,1,1024]{3,1,2,0:T(8,128)S(1)} copy(f32[3,64,1,1024]{3,2,1,0:T(1,128)} %param.11) | data formatting | bytes 1572864
  1.4 0.0 copy-done
  1.4 0.0 copy-done.1
  1.4 0.0 copy-done.4
  1.5 0.0 copy-done.5
  1.5 0.0 copy-done.6
  1.5 0.0 copy-done.7
  1.6 1.7 %shard_map.109 = f32[32,48,128]{2,1,0:T(8,128)} custom-call(f32[192,1024]{1,0:T(8,128)S(1)} %bitcast.3, bf16[256,256]{1,0:T(8,128)(2,1)S(1)} %copy-done.7, bf16[256,256]{1,0:T(8,128)(2,1)S(1)} %copy-done.6, bf16[256,256]{1,0:T(8,128)(2,1)S(1)} %copy-done.5, bf16[256,256]{1,0:T(8,128)(2,1)S(1)} %copy-done.4, bf16[512,512]{1,0:T(8,128)(2,1)S(1)} %copy-done.1, ...), custom_call_target="tpu_custom_call" | custom-call | tf_op jit(solution)/shard_map/pallas_call | solution.py:486
  3.3 0.0 copy-start.9
  3.3 0.0 copy-start.2
  3.3 0.0 copy-start.3
  3.3 0.0 copy-start.8
  3.3 7.3 %all-to-all-start = ((f32[32,48,128]{2,1,0:T(8,128)}), f32[32,48,128]{2,1,0:T(8,128)S(1)}, u32[]{:S(2)}, u32[]{:S(2)}) async-start(f32[32,48,128]{2,1,0:T(8,128)} %shard_map.109), calls=%async_computation | async-start | bytes 1572864 | tf_op jit(solution)/shard_map/all_to_all | solution.py:455
  10.6 0.0 copy-done.9
  10.7 0.1 fusion.1
  10.7 0.1 fusion
  10.8 0.1 div.14.weight_ref
  10.9 20.3 %all-to-all-done.in_ref = f32[32,48,128]{2,1,0:T(8,128)S(1)} async-done(((f32[32,48,128]{2,1,0:T(8,128)}), f32[32,48,128]{2,1,0:T(8,128)S(1)}, u32[]{:S(2)}, u32[]{:S(2)}) %all-to-all-start) | async-done | bytes 786464 | tf_op jit(solution)/shard_map/all_to_all | solution.py:455
  31.2 0.0 copy-done.2
  31.2 0.0 copy-done.3
  31.2 0.0 copy-done.8
  31.2 3.3 %shard_map.110 = f32[32,96,128]{2,1,0:T(8,128)S(1)} custom-call(s32[1]{0:T(128)} %bitcast.me_ref, f32[4]{0:T(128)S(1)} %div.14.weight_ref, f32[32,48,128]{2,1,0:T(8,128)S(1)} %all-to-all-done.in_ref, bf16[512,512]{1,0:T(8,128)(2,1)S(1)} %copy-done.3, bf16[512,512]{1,0:T(8,128)(2,1)S(1)} %copy-done.2, f32[8,256]{1,0:T(8,128)S(1)} %copy-done.8), custom_call_target="tpu_custom_call" | custom-call | tf_op jit(solution)/shard_map/pallas_call | solution.py:499
  34.6 40.9 %all_to_all.10.in_ref = f32[32,96,128]{2,1,0:T(8,128)S(1)} all-to-all(f32[32,96,128]{2,1,0:T(8,128)S(1)} %shard_map.110), channel_id=1, replica_groups=mesh['px'=16,'py'=2] {'px','py'}, dimensions={0} | all-to-all | bytes 3145728 | tf_op jit(solution)/shard_map/all_to_all | solution.py:455
  75.4 2.3 %shard_map.111 = f32[4,3,32,1024]{3,2,1,0:T(8,128)} custom-call(f32[32,96,128]{2,1,0:T(8,128)S(1)} %all_to_all.10.in_ref, bf16[256,256]{1,0:T(8,128)(2,1)S(1)} %copy-done.7, bf16[256,256]{1,0:T(8,128)(2,1)S(1)} %copy-done.6, bf16[256,256]{1,0:T(8,128)(2,1)S(1)} %copy-done.5, bf16[256,256]{1,0:T(8,128)(2,1)S(1)} %copy-done.4, bf16[512,512]{1,0:T(8,128)(2,1)S(1)} %copy-done.1, ...), custom_call_target="tpu_custom_call" | custom-call | tf_op jit(solution)/shard_map/pallas_call | solution.py:507
  (1 shorter events, 0.0 us)
Async XLA Ops:
  0.0 1.4 %copy-start = (bf16[512,512]{1,0:T(8,128)(2,1)S(1)}, bf16[512,512]{1,0:T(8,128)(2,1)}, u32[]{:S(2)}) copy-start(bf16[512,512]{1,0:T(8,128)(2,1)} %constant.37.clone.o_l) | copy-start | bytes 1572868
  0.0 1.4 %copy-start.1 = (bf16[512,512]{1,0:T(8,128)(2,1)S(1)}, bf16[512,512]{1,0:T(8,128)(2,1)}, u32[]{:S(2)}) copy-start(bf16[512,512]{1,0:T(8,128)(2,1)} %constant.36.clone.o_h) | copy-start | bytes 1572868
  0.0 1.5 %copy-start.4 = (bf16[256,256]{1,0:T(8,128)(2,1)S(1)}, bf16[256,256]{1,0:T(8,128)(2,1)}, u32[]{:S(2)}) copy-start(bf16[256,256]{1,0:T(8,128)(2,1)} %constant.35.clone.m_l) | copy-start | bytes 393220
  0.0 1.5 %copy-start.5 = (bf16[256,256]{1,0:T(8,128)(2,1)S(1)}, bf16[256,256]{1,0:T(8,128)(2,1)}, u32[]{:S(2)}) copy-start(bf16[256,256]{1,0:T(8,128)(2,1)} %constant.34.clone.m_h) | copy-start | bytes 393220
  0.0 1.5 %copy-start.6 = (bf16[256,256]{1,0:T(8,128)(2,1)S(1)}, bf16[256,256]{1,0:T(8,128)(2,1)}, u32[]{:S(2)}) copy-start(bf16[256,256]{1,0:T(8,128)(2,1)} %constant.33.clone.e_l) | copy-start | bytes 393220
  0.0 1.6 %copy-start.7 = (bf16[256,256]{1,0:T(8,128)(2,1)S(1)}, bf16[256,256]{1,0:T(8,128)(2,1)}, u32[]{:S(2)}) copy-start(bf16[256,256]{1,0:T(8,128)(2,1)} %constant.32.clone.e_h) | copy-start | bytes 393220
  3.3 7.4 %copy-start.9 = (s32[2]{0:T(128)S(1)}, s32[2]{0:T(128)}, u32[]{:S(2)}) copy-start(s32[2]{0:T(128)} %param.12) | copy-start | bytes 28
  3.3 27.9 %copy-start.2 = (bf16[512,512]{1,0:T(8,128)(2,1)S(1)}, bf16[512,512]{1,0:T(8,128)(2,1)}, u32[]{:S(2)}) copy-start(bf16[512,512]{1,0:T(8,128)(2,1)} %constant.39.clone.t_l) | copy-start | bytes 1572868
  3.3 27.9 %copy-start.3 = (bf16[512,512]{1,0:T(8,128)(2,1)S(1)}, bf16[512,512]{1,0:T(8,128)(2,1)}, u32[]{:S(2)}) copy-start(bf16[512,512]{1,0:T(8,128)(2,1)} %constant.38.clone.t_h) | copy-start | bytes 1572868
  3.3 27.9 %copy-start.8 = (f32[8,256]{1,0:T(8,128)S(1)}, f32[8,256]{1,0:T(8,128)}, u32[]{:S(2)}) copy-start(f32[8,256]{1,0:T(8,128)} %constant.40.clone.w_ref) | copy-start | bytes 24580
  3.3 27.9 %all-to-all-start = ((f32[32,48,128]{2,1,0:T(8,128)}), f32[32,48,128]{2,1,0:T(8,128)S(1)}, u32[]{:S(2)}, u32[]{:S(2)}) async-start(f32[32,48,128]{2,1,0:T(8,128)} %shard_map.109), calls=%async_computation | async-start | bytes 1572864 | tf_op jit(solution)/shard_map/all_to_all | solution.py:455

commit v2 on v1

--- a/solution.py
+++ b/solution.py
@@ -223,7 +223,7 @@
 NN = ((1,), (0,))
 
 
-def span_kernel(share, v_ref, e_h, e_l, m_h, m_l, o_h, o_l, out_ref):
+def span_stage(share, v_ref, e_h, e_l, m_h, m_l, o_h, o_l, out_ref):
     values = v_ref[...]
     rows = values.shape[0] // 3
     values = jnp.concatenate((values, values[2 * rows :]), 0)
@@ -244,8 +244,7 @@
     out_ref[:, 2 * share :] = third.reshape(-1, share, 128)
 
 
-def stream_kernel(share, planes, me_ref, weight_ref, in_ref, t_h, t_l, w_ref, out_ref):
-    first_device = me_ref[0] == 0
+def stream_stage(share, planes, first_device, band_ref, in_ref, t_h, t_l, w_ref, span_cells, out_ref, send_part):
     px_count = in_ref.shape[0] // planes
     columns = px_count // 2
     group_cols = columns // 4
@@ -317,156 +316,216 @@
     row = lax.broadcasted_iota(jnp.int32, (4 * share, quarter), 0)
     single = jnp.logical_and(row % share == 0, first_device)
     multiplier = jnp.where(single, 1.0, 2.0)
-    own, mutual = [], []
-    for left, right in PAIR_LIST:
-        real_sum, imag_sum = [None] * NB, [None] * NB
+    onehot, scale = [], []
+    for b in range(NB):
+        hot = [
+            jnp.where(jnp.full((4 * share, quarter), band_ref[y], jnp.int32) == b, 1.0, 0.0)
+            for y in range(planes)
+        ]
+        onehot.append(hot)
+        scale.append(multiplier / (sum(hot[1:], hot[0]) * (span_cells * math.sqrt(span_cells))))
+
+    def banded(left, right, b):
+        real_sum = imag_sum = None
         for y in range(planes):
             lr, li = field[left][y]
             rr, ri = field[right][y]
-            real = lr * rr + li * ri
-            imag = None if left == right else lr * ri - li * rr
-            for b in range(NB):
-                weight = weight_ref[y * NB + b]
-                add = weight * real
-                real_sum[b] = add if y == 0 else real_sum[b] + add
-                if imag is not None:
-                    add = weight * imag
-                    imag_sum[b] = add if y == 0 else imag_sum[b] + add
-        for b in range(NB):
-            if left == right:
-                own.append(real_sum[b] * multiplier)
-            else:
-                mutual.append(
-                    jnp.concatenate((real_sum[b] * multiplier, imag_sum[b] * multiplier), 1)
-                )
+            add = onehot[b][y] * (lr * rr + li * ri)
+            real_sum = add if y == 0 else real_sum + add
+            if left != right:
+                add = onehot[b][y] * (lr * ri - li * rr)
+                imag_sum = add if y == 0 else imag_sum + add
+        if left == right:
+            return real_sum * scale[b]
+        return jnp.concatenate((real_sum * scale[b], imag_sum * scale[b]), 1)
+
     own_table = (t_h[:, :quarter], t_l[:, :quarter])
-    own_back = three_dots(split_value(jnp.concatenate(own, 0)), own_table, NT)
-    mutual_back = three_dots(split_value(jnp.concatenate(mutual, 0)), table, NT)
-    lines = []
-    own_at = mutual_at = 0
-    for left, right in PAIR_LIST:
-        for b in range(NB):
-            if left == right:
-                back = own_back[own_at * 4 * share : (own_at + 1) * 4 * share]
-                own_at += 1
-            else:
-                back = mutual_back[mutual_at * 4 * share : (mutual_at + 1) * 4 * share]
-                mutual_at += 1
-            turned = []
-            for k1 in range(4):
-                real = back[k1 * share : (k1 + 1) * share, :quarter]
-                imag = back[k1 * share : (k1 + 1) * share, quarter:]
-                if k1:
-                    cosine, sine = w_ref[k1 : k1 + 1], w_ref[4 + k1 : 5 + k1]
-                    real, imag = real * cosine - imag * sine, imag * cosine + real * sine
-                turned.append((real, imag))
-            s02 = [turned[0][i] + turned[2][i] for i in range(2)]
-            d02 = [turned[0][i] - turned[2][i] for i in range(2)]
-            s13 = [turned[1][i] + turned[3][i] for i in range(2)]
-            d13 = [turned[1][i] - turned[3][i] for i in range(2)]
-            real = (s02[0] + s13[0], d02[0] - d13[1], s02[0] - s13[0], d02[0] + d13[1])
-            imag = (s02[1] + s13[1], d02[1] + d13[0], s02[1] - s13[1], d02[1] - d13[0])
-            lines.append((real, imag))
+
+    def lines_of(members):
+        value = [banded(*PAIR_LIST[m // NB], m % NB) for m in members]
+        result = [None] * len(members)
+        for columns_in, used in ((quarter, own_table), (2 * quarter, table)):
+            chosen = [n for n in range(len(members)) if value[n].shape[1] == columns_in]
+            if not chosen:
+                continue
+            joined = jnp.concatenate([value[n] for n in chosen], 0)
+            whole = three_dots(split_value(joined), used, NT)
+            for place, n in enumerate(chosen):
+                result[n] = spread(whole[place * 4 * share : (place + 1) * 4 * share])
+        return result
+
+    def spread(back):
+        turned = []
+        for k1 in range(4):
+            real = back[k1 * share : (k1 + 1) * share, :quarter]
+            imag = back[k1 * share : (k1 + 1) * share, quarter:]
+            if k1:
+                cosine, sine = w_ref[k1 : k1 + 1], w_ref[4 + k1 : 5 + k1]
+                real, imag = real * cosine - imag * sine, imag * cosine + real * sine
+            turned.append((real, imag))
+        s02 = [turned[0][i] + turned[2][i] for i in range(2)]
+        d02 = [turned[0][i] - turned[2][i] for i in range(2)]
+        s13 = [turned[1][i] + turned[3][i] for i in range(2)]
+        d13 = [turned[1][i] - turned[3][i] for i in range(2)]
+        real = (s02[0] + s13[0], d02[0] - d13[1], s02[0] - s13[0], d02[0] + d13[1])
+        imag = (s02[1] + s13[1], d02[1] + d13[0], s02[1] - s13[1], d02[1] - d13[0])
+        return real, imag
+
     width = 4 * quarter // in_ref.shape[0]
     groups = 128 // width
-    per_group = len(lines) // groups
+    per_group = out_ref.shape[0]
     lane = lax.broadcasted_iota(jnp.int32, (share, 128), 1)
     for i in range(per_group):
+        lines = lines_of([g * per_group + i for g in range(groups)])
         for ri in range(2):
-            at = (2 * i + ri) * share
+            at = ri * share
             for q in range(4 * quarter // 128):
                 j, inside = q * 128 // quarter, q * 128 % quarter
-                tiles = [
-                    lines[g * per_group + i][ri][j][:, inside : inside + 128]
-                    for g in range(groups)
-                ]
+                tiles = [lines[g][ri][j][:, inside : inside + 128] for g in range(groups)]
                 for t in range(groups):
                     packed = None
                     for g in range(groups):
                         shift = (g - t) * width % 128
                         tile = pltpu.roll(tiles[g], shift, 1) if shift else tiles[g]
                         packed = tile if g == 0 else jnp.where(lane >= g * width, tile, packed)
-                    out_ref[q * groups + t, at : at + share] = packed
-
-
-def back_kernel(share, in_ref, e_h, e_l, m_h, m_l, o_h, o_l, out_ref):
-    devices = in_ref.shape[0]
-    groups, per_group, width, length = out_ref.shape
+                    out_ref[i, q * groups + t, at : at + share] = packed
+        send_part(i)
+
+
+def back_stage(share, i, in_ref, e_h, e_l, m_h, m_l, o_h, o_l, out_ref):
+    devices = in_ref.shape[1]
+    _, groups, width, length = out_ref.shape
     quarter, eighth = length // 4, length // 8
-    for i in range(per_group):
-        at = 2 * i * share
-        real = in_ref[:, at : at + share].reshape(devices * share, 128).T
-        imag = in_ref[:, at + share : at + 2 * share].reshape(devices * share, 128).T
-
-        def both(start, stop):
-            return split_value(jnp.concatenate((real[:, start:stop], imag[:, start:stop]), 1))
-
-        even = three_dots(both(0, eighth), (e_h[...], e_l[...]), NN)
-        middle = three_dots(both(eighth, quarter), (m_h[...], m_l[...]), NN)
-        odd = three_dots(both(quarter, 2 * quarter), (o_h[...], o_l[...]), NN)
-        plus, minus = even + middle, even - middle
-        first, second = odd[:, :quarter], odd[:, quarter:]
-        for j, line in enumerate((plus + first, minus + second, plus - first, minus - second)):
-            out_ref[:, i, :, j * quarter : (j + 1) * quarter] = line.reshape(groups, width, quarter)
-
-
-def swap_kernel(px_count, py_count, in_ref, out_ref, send_sem, recv_sem, own_sem):
+    real = in_ref[i, :, :share].reshape(devices * share, 128).T
+    imag = in_ref[i, :, share : 2 * share].reshape(devices * share, 128).T
+
+    def both(start, stop):
+        return split_value(jnp.concatenate((real[:, start:stop], imag[:, start:stop]), 1))
+
+    even = three_dots(both(0, eighth), (e_h[...], e_l[...]), NN)
+    middle = three_dots(both(eighth, quarter), (m_h[...], m_l[...]), NN)
+    odd = three_dots(both(quarter, 2 * quarter), (o_h[...], o_l[...]), NN)
+    plus, minus = even + middle, even - middle
+    first, second = odd[:, :quarter], odd[:, quarter:]
+    for j, line in enumerate((plus + first, minus + second, plus - first, minus - second)):
+        out_ref[i, :, :, j * quarter : (j + 1) * quarter] = line.reshape(groups, width, quarter)
+
+
+def flip_bits(index, bits):
+    moved, bit = index, 1
+    while bit <= bits:
+        if bits & bit:
+            moved = moved + bit * (1 - 2 * ((index // bit) % 2))
+        bit *= 2
+    return moved
+
+
+def whole_kernel(
+    px_count,
+    py_count,
+    share,
+    band_ref,
+    v_far,
+    e_h_far,
+    e_l_far,
+    m_h_far,
+    m_l_far,
+    o_h_far,
+    o_l_far,
+    t_h_far,
+    t_l_far,
+    w_far,
+    out_ref,
+    v_ref,
+    e_h,
+    e_l,
+    m_h,
+    m_l,
+    o_h,
+    o_l,
+    t_h,
+    t_l,
+    w_ref,
+    spec_out,
+    spec_in,
+    back_out,
+    back_in,
+    result,
+    send_sem,
+    recv_sem,
+    own_sem,
+    table_sem,
+    out_sem,
+):
+    far = (v_far, o_h_far, o_l_far, e_h_far, e_l_far, m_h_far, m_l_far)
+    near = (v_ref, o_h, o_l, e_h, e_l, m_h, m_l)
+    far, near = far + (t_h_far, t_l_far, w_far), near + (t_h, t_l, w_ref)
+    loads = [
+        pltpu.make_async_copy(far[n], near[n], table_sem.at[n]) for n in range(len(far))
+    ]
+    for load in loads:
+        load.start()
     px, py = lax.axis_index("px"), lax.axis_index("py")
     me = px * py_count + py
     count = px_count * py_count
+    parts = back_out.shape[0]
     barrier = pltpu.get_barrier_semaphore()
-
-    def peer(step):
-        other_px = lax.rem(px + step // py_count, px_count)
-        other_py = lax.rem(py + step % py_count, py_count)
-        return other_px, other_py
-
-    for step in range(1, count):
+    steps = list(range(count - 1, 0, -1))
+    peers = {s: (flip_bits(px, s // py_count), flip_bits(py, s % py_count)) for s in steps}
+    for s in steps:
         pl.semaphore_signal(
-            barrier, inc=1, device_id=peer(step), device_id_type=pl.DeviceIdType.MESH
-        )
-    own = pltpu.make_async_copy(in_ref.at[me], out_ref.at[me], own_sem)
-    own.start()
+            barrier, inc=1, device_id=peers[s], device_id_type=pl.DeviceIdType.MESH
+        )
+    def swap(lane, source, target):
+        own = pltpu.make_async_copy(source.at[me], target.at[me], own_sem.at[lane])
+        copies = []
+        for s in steps:
+            copy = pltpu.make_async_remote_copy(
+                src_ref=source.at[peers[s][0] * py_count + peers[s][1]],
+                dst_ref=target.at[me],
+                send_sem=send_sem.at[lane, s],
+                recv_sem=recv_sem.at[lane, s],
+                device_id=peers[s],
+                device_id_type=pl.DeviceIdType.MESH,
+            )
+            copy.start()
+            copies.append(copy)
+        own.start()
+        return own, copies
+
+    def arrive(moves):
+        moves[0].wait()
+        for copy in moves[1]:
+            copy.wait_recv()
+
+    for load in loads[:7]:
+        load.wait()
+    span_stage(share, v_ref, e_h, e_l, m_h, m_l, o_h, o_l, spec_out)
     pl.semaphore_wait(barrier, count - 1)
-    copies = []
-    order = sorted(range(1, count), key=lambda s: -min(s, count - s))
-    for step in order:
-        other = peer(step)
-        copy = pltpu.make_async_remote_copy(
-            src_ref=in_ref.at[other[0] * py_count + other[1]],
-            dst_ref=out_ref.at[me],
-            send_sem=send_sem.at[step],
-            recv_sem=recv_sem.at[step],
-            device_id=other,
-            device_id_type=pl.DeviceIdType.MESH,
-        )
-        copy.start()
-        copies.append(copy)
-    own.wait()
-    for copy in copies:
-        copy.wait()
-
-
-REMOTE = False
-
-
-def swap_blocks(value, px_count, py_count, collective):
-    if not REMOTE:
-        return lax.all_to_all(value, ("px", "py"), split_axis=0, concat_axis=0, tiled=True)
-    count = px_count * py_count
-    space = pl.BlockSpec(memory_space=pltpu.VMEM)
-    return pl.pallas_call(
-        functools.partial(swap_kernel, px_count, py_count),
-        out_shape=jax.ShapeDtypeStruct(value.shape, value.dtype),
-        in_specs=[space],
-        out_specs=space,
-        scratch_shapes=[
-            pltpu.SemaphoreType.DMA((count,)),
-            pltpu.SemaphoreType.DMA((count,)),
-            pltpu.SemaphoreType.DMA,
-        ],
-        compiler_params=pltpu.CompilerParams(collective_id=collective, has_side_effects=True),
-    )(value)
+    moves = [swap(0, spec_out, spec_in)]
+    for load in loads[7:]:
+        load.wait()
+    arrive(moves[0])
+
+    def send_part(i):
+        moves.append(swap(1 + i, back_out.at[i], back_in.at[i]))
+
+    cells = float(v_ref.shape[1] * 4 * w_ref.shape[1])
+    stream_stage(
+        share, py_count, me == 0, band_ref, spec_in, t_h, t_l, w_ref, cells, back_out, send_part
+    )
+    stores = []
+    for i in range(parts):
+        arrive(moves[1 + i])
+        back_stage(share, i, back_in, e_h, e_l, m_h, m_l, o_h, o_l, result)
+        store = pltpu.make_async_copy(result.at[i], out_ref.at[:, i], out_sem.at[i])
+        store.start()
+        stores.append(store)
+    for _, copies in moves:
+        for copy in copies:
+            copy.wait_send()
+    for store in stores:
+        store.wait()
 
 
 def register_device(velocity, band_of):
@@ -478,39 +537,34 @@
     share = span // 2 // count
     width = stream // count
     groups = 128 // width
-    per_group = len(PAIR_LIST) * NB // groups
-    vmem = pl.BlockSpec(memory_space=pltpu.VMEM)
+    parts = len(PAIR_LIST) * NB // groups
     smem = pl.BlockSpec(memory_space=pltpu.SMEM)
-    tables = span_tables(span)
-    params = pltpu.CompilerParams(vmem_limit_bytes=48 * 1024 * 1024)
-    spec = pl.pallas_call(
-        functools.partial(span_kernel, share),
-        out_shape=jax.ShapeDtypeStruct((count, 3 * share, 128), jnp.float32),
-        in_specs=[vmem] * 7,
-        out_specs=vmem,
-        compiler_params=params,
-    )(velocity.reshape(3 * rows_x, span), *tables)
-    spec = swap_blocks(spec, px_count, py_count, 0)
-    band_ids = lax.iota(jnp.int32, NB)
-    onehot = (band_of[:, None] == band_ids[None, :]).astype(jnp.float32)
-    cells = float(stream * span)
-    weight = onehot / (jnp.sum(onehot, 0)[None, :] * (cells * math.sqrt(cells)))
-    me = (lax.axis_index("px") * py_count + lax.axis_index("py")).astype(jnp.int32)
-    back = pl.pallas_call(
-        functools.partial(stream_kernel, share, py_count),
-        out_shape=jax.ShapeDtypeStruct((count, 2 * per_group * share, 128), jnp.float32),
-        in_specs=[smem, smem] + [vmem] * 4,
-        out_specs=vmem,
-        compiler_params=params,
-    )(me.reshape(1), weight.reshape(-1), spec, *stream_tables(stream))
-    back = swap_blocks(back, px_count, py_count, 1)
+    far = pl.BlockSpec(memory_space=pl.ANY)
+    spec_shape = (count, 3 * share, 128)
+    back_shape = (parts, count, 2 * share, 128)
+    operands = (velocity.reshape(3 * rows_x, span),) + span_tables(span) + stream_tables(stream)
     out = pl.pallas_call(
-        functools.partial(back_kernel, share),
-        out_shape=jax.ShapeDtypeStruct((groups, per_group, width, span), jnp.float32),
-        in_specs=[vmem] * 7,
-        out_specs=vmem,
-        compiler_params=params,
-    )(back, *tables)
+        functools.partial(whole_kernel, px_count, py_count, share),
+        out_shape=jax.ShapeDtypeStruct((groups, parts, width, span), jnp.float32),
+        in_specs=[smem] + [far] * len(operands),
+        out_specs=far,
+        scratch_shapes=[pltpu.VMEM(x.shape, x.dtype) for x in operands]
+        + [
+            pltpu.VMEM(spec_shape, jnp.float32),
+            pltpu.VMEM(spec_shape, jnp.float32),
+            pltpu.VMEM(back_shape, jnp.float32),
+            pltpu.VMEM(back_shape, jnp.float32),
+            pltpu.VMEM((parts, groups, width, span), jnp.float32),
+            pltpu.SemaphoreType.DMA((1 + parts, count)),
+            pltpu.SemaphoreType.DMA((1 + parts, count)),
+            pltpu.SemaphoreType.DMA((1 + parts,)),
+            pltpu.SemaphoreType.DMA((len(operands),)),
+            pltpu.SemaphoreType.DMA((parts,)),
+        ],
+        compiler_params=pltpu.CompilerParams(
+            collective_id=0, has_side_effects=True, vmem_limit_bytes=60 * 1024 * 1024
+        ),
+    )(band_of, *operands)
     return out.reshape(len(PAIR_LIST), NB, width, span)
 
 
@@ -524,6 +578,8 @@
         comps == 3
         and rows_x == 64
         and planes == 1
+        and px_count & (px_count - 1) == 0
+        and py_count & (py_count - 1) == 0
         and px_count % 8 == 0
         and span % 1024 == 0
         and stream % 512 == 0

time: 78.6 us -> 69.7 us (0.89)
  Pallas kernels: 7.36 us -> 64.7 us
  blocking collectives: 40.9 us -> 0 us
  waiting for transfers between devices: 20.3 us -> 0 us
  starting transfers between devices: 7.34 us -> 0 us
  local copies, waits for them, and re-layouts: 1.64 us -> 4.88 us
    pallas_call x3 -> x1, Pallas kernels: 7.36 us -> 64.7 us  [register_device(): pl.pallas_call(functools.partial(whole_kernel, px_count, py_count, share)...]
    all_to_all x1 -> x0, blocking collectives: 40.9 us -> none  [swap_blocks(): lax.all_to_all(value, ('px', 'py'), split_axis=0, concat_axis=0, tiled=True)]
    all_to_all x1 -> x0, waiting for transfers between devices: 20.3 us -> none  [swap_blocks(): lax.all_to_all(value, ('px', 'py'), split_axis=0, concat_axis=0, tiled=True)]
    all_to_all x1 -> x0, starting transfers between devices: 7.34 us -> none  [swap_blocks(): lax.all_to_all(value, ('px', 'py'), split_axis=0, concat_axis=0, tiled=True)]
    unnamed x21 -> x2, local copies, waits for them, and re-layouts: 1.55 us -> 4.88 us
  transfers between devices with their start and end apart: 1 -> 0, of which waited for: 1 -> 0; matrix products, arithmetic and copies ran while one was open for 0% -> 0% of each run, Pallas kernels for 0% -> 0%
where the time goes in v2:
time: 69.7 us; the launch traced here: 69.6 us
  Pallas kernels  64.7 us (93%)
  local copies, waits for them, and re-layouts  4.88 us (7%)
    pallas_call x1, Pallas kernels, register_device(): pl.pallas_call(functools.partial(whole_kernel, px_count, py_count, share)...  64.7 us
    unnamed x2, local copies, waits for them, and re-layouts  4.88 us

profile of v2, /device:TPU:0, one launch (start us, length us, event | category | flops | bytes accessed | tf_op | source)
XLA Modules:
  0.0 69.6 jit_solution(17530030349384018383)
XLA Ops:
  0.0 2.2 %copy.12 = f32[3,64,1,1024]{3,1,2,0:T(8,128)} copy(f32[3,64,1,1024]{3,2,1,0:T(1,128)} %param.11) | data formatting | bytes 1572864
  2.2 64.7 %shard_map.109 = f32[4,3,32,1024]{3,2,1,0:T(8,128)} custom-call(s32[2]{0:T(128)} %band_ref.1, f32[192,1024]{1,0:T(8,128)} %bitcast.3, bf16[256,256]{1,0:T(8,128)(2,1)} %constant.18.clone.e_h_far, bf16[256,256]{1,0:T(8,128)(2,1)} %constant.19.clone.e_l_far, bf16[256,256]{1,0:T(8,128)(2,1)} %constant.20.clone.m_h_far, ...), custom_call_target="tpu_custom_call" | custom-call | tf_op jit(solution)/shard_map/pallas_call | solution.py:546
  66.8 2.7 %copy.14 = f32[6,2,32,1024]{3,2,1,0:T(8,128)} copy(f32[6,2,32,1024]{3,2,1,0:T(8,128)} %bitcast.2) | data formatting | bytes 3145728

commit v3 on v2

--- a/solution.py
+++ b/solution.py
@@ -425,27 +425,11 @@
     py_count,
     share,
     band_ref,
-    v_far,
-    e_h_far,
-    e_l_far,
-    m_h_far,
-    m_l_far,
-    o_h_far,
-    o_l_far,
-    t_h_far,
-    t_l_far,
-    w_far,
+    v_ref,
+    table_far,
+    w_ref,
     out_ref,
-    v_ref,
-    e_h,
-    e_l,
-    m_h,
-    m_l,
-    o_h,
-    o_l,
-    t_h,
-    t_l,
-    w_ref,
+    tables,
     spec_out,
     spec_in,
     back_out,
@@ -457,12 +441,21 @@
     table_sem,
     out_sem,
 ):
-    far = (v_far, o_h_far, o_l_far, e_h_far, e_l_far, m_h_far, m_l_far)
-    near = (v_ref, o_h, o_l, e_h, e_l, m_h, m_l)
-    far, near = far + (t_h_far, t_l_far, w_far), near + (t_h, t_l, w_ref)
+    quarter = v_ref.shape[1] // 4
+    cuts = (0, 2 * quarter, 6 * quarter, 8 * quarter, 10 * quarter)
     loads = [
-        pltpu.make_async_copy(far[n], near[n], table_sem.at[n]) for n in range(len(far))
+        pltpu.make_async_copy(
+            table_far.at[start:stop], tables.at[start:stop], table_sem.at[n]
+        )
+        for n, (start, stop) in enumerate(zip(cuts[:-1], cuts[1:]))
     ]
+    e_h, m_h = tables.at[:quarter, :quarter], tables.at[:quarter, quarter:]
+    e_l = tables.at[quarter : 2 * quarter, :quarter]
+    m_l = tables.at[quarter : 2 * quarter, quarter:]
+    o_h = tables.at[2 * quarter : 4 * quarter]
+    o_l = tables.at[4 * quarter : 6 * quarter]
+    t_h = tables.at[6 * quarter : 8 * quarter]
+    t_l = tables.at[8 * quarter :]
     for load in loads:
         load.start()
     px, py = lax.axis_index("px"), lax.axis_index("py")
@@ -498,12 +491,12 @@
         for copy in moves[1]:
             copy.wait_recv()
 
-    for load in loads[:7]:
+    for load in loads[:2]:
         load.wait()
     span_stage(share, v_ref, e_h, e_l, m_h, m_l, o_h, o_l, spec_out)
     pl.semaphore_wait(barrier, count - 1)
     moves = [swap(0, spec_out, spec_in)]
-    for load in loads[7:]:
+    for load in loads[2:]:
         load.wait()
     arrive(moves[0])
 
@@ -538,18 +531,22 @@
     width = stream // count
     groups = 128 // width
     parts = len(PAIR_LIST) * NB // groups
+    vmem = pl.BlockSpec(memory_space=pltpu.VMEM)
     smem = pl.BlockSpec(memory_space=pltpu.SMEM)
     far = pl.BlockSpec(memory_space=pl.ANY)
     spec_shape = (count, 3 * share, 128)
     back_shape = (parts, count, 2 * share, 128)
-    operands = (velocity.reshape(3 * rows_x, span),) + span_tables(span) + stream_tables(stream)
+    e_h, e_l, m_h, m_l, o_h, o_l = span_tables(span)
+    t_h, t_l, twiddle = stream_tables(stream)
+    even = [np.concatenate(pair, 1) for pair in ((e_h, m_h), (e_l, m_l))]
+    tables = np.concatenate(even + [o_h, o_l, t_h, t_l], 0)
     out = pl.pallas_call(
         functools.partial(whole_kernel, px_count, py_count, share),
         out_shape=jax.ShapeDtypeStruct((groups, parts, width, span), jnp.float32),
-        in_specs=[smem] + [far] * len(operands),
+        in_specs=[smem, vmem, far, vmem],
         out_specs=far,
-        scratch_shapes=[pltpu.VMEM(x.shape, x.dtype) for x in operands]
-        + [
+        scratch_shapes=[
+            pltpu.VMEM(tables.shape, tables.dtype),
             pltpu.VMEM(spec_shape, jnp.float32),
             pltpu.VMEM(spec_shape, jnp.float32),
             pltpu.VMEM(back_shape, jnp.float32),
@@ -558,13 +555,13 @@
             pltpu.SemaphoreType.DMA((1 + parts, count)),
             pltpu.SemaphoreType.DMA((1 + parts, count)),
             pltpu.SemaphoreType.DMA((1 + parts,)),
-            pltpu.SemaphoreType.DMA((len(operands),)),
+            pltpu.SemaphoreType.DMA((4,)),
             pltpu.SemaphoreType.DMA((parts,)),
         ],
         compiler_params=pltpu.CompilerParams(
-            collective_id=0, has_side_effects=True, vmem_limit_bytes=60 * 1024 * 1024
+            collective_id=0, has_side_effects=True, vmem_limit_bytes=49152 * 1024
         ),
-    )(band_of, *operands)
+    )(band_of, velocity.reshape(3 * rows_x, span), tables, twiddle)
     return out.reshape(len(PAIR_LIST), NB, width, span)
 
 
@@ -582,7 +579,7 @@
         and py_count & (py_count - 1) == 0
         and px_count % 8 == 0
         and span % 1024 == 0
-        and stream % 512 == 0
+        and stream == span
         and stream == width * count
         and span == 2 * share * count
         and share % 8 == 0

time: 69.7 us -> 68.2 us (0.978)
  Pallas kernels: 64.7 us -> 63.9 us
    pallas_call x1, Pallas kernels: 64.7 us -> 63.9 us  [register_device(): pl.pallas_call(functools.partial(whole_kernel, px_count, py_count, share)...]
    unnamed x2 -> x8, local copies, waits for them, and re-layouts: 4.88 us -> 4.19 us
where the time goes in v3:
time: 68.2 us; the launch traced here: 68.1 us
  Pallas kernels  63.9 us (94%)
  local copies, waits for them, and re-layouts  4.19 us (6%)
    pallas_call x1, Pallas kernels, register_device(): pl.pallas_call(functools.partial(whole_kernel, px_count, py_count, share)...  63.9 us
    unnamed x8, local copies, waits for them, and re-layouts  4.19 us

profile of v3, /device:TPU:0, one launch (start us, length us, event | category | flops | bytes accessed | tf_op | source)
XLA Modules:
  0.0 68.1 jit_solution(3944423028367903820)
XLA Ops:
  0.0 0.0 copy-start.1
  0.0 0.0 copy-start.2
  0.0 1.3 %copy.5 = f32[3,64,1,1024]{3,1,2,0:T(8,128)S(1)} copy(f32[3,64,1,1024]{3,2,1,0:T(1,128)} %param.4) | data formatting | bytes 1572864
  1.3 0.0 copy-done.1
  1.3 0.0 copy-done.2
  1.3 0.0 copy-start
  1.3 1.7 %copy-done = bf16[2560,512]{1,0:T(8,128)(2,1)S(1)} copy-done((bf16[2560,512]{1,0:T(8,128)(2,1)S(1)}, bf16[2560,512]{1,0:T(8,128)(2,1)}, u32[]{:S(2)}) %copy-start) | copy-done | bytes 2621464
  3.1 63.9 %shard_map.46 = f32[4,3,32,1024]{3,2,1,0:T(8,128)S(1)} custom-call(s32[2]{0:T(128)S(1)} %copy-done.2, f32[192,1024]{1,0:T(8,128)S(1)} %bitcast.3, bf16[2560,512]{1,0:T(8,128)(2,1)S(1)} %copy-done, f32[8,256]{1,0:T(8,128)S(1)} %copy-done.1), custom_call_target="tpu_custom_call" | custom-call | tf_op jit(solution)/shard_map/pallas_call | solution.py:543
  66.9 1.1 %copy.7 = f32[6,2,32,1024]{3,2,1,0:T(8,128)} copy(f32[6,2,32,1024]{3,2,1,0:T(8,128)S(1)} %bitcast.2) | data formatting | bytes 3145728
Async XLA Ops:
  0.0 1.3 %copy-start.1 = (f32[8,256]{1,0:T(8,128)S(1)}, f32[8,256]{1,0:T(8,128)}, u32[]{:S(2)}) copy-start(f32[8,256]{1,0:T(8,128)} %constant.5.clone.w_ref) | copy-start | bytes 24580
  0.0 1.3 %copy-start.2 = (s32[2]{0:T(128)S(1)}, s32[2]{0:T(128)}, u32[]{:S(2)}) copy-start(s32[2]{0:T(128)} %band_ref.1) | copy-start | bytes 28
  1.3 1.7 %copy-start = (bf16[2560,512]{1,0:T(8,128)(2,1)S(1)}, bf16[2560,512]{1,0:T(8,128)(2,1)}, u32[]{:S(2)}) copy-start(bf16[2560,512]{1,0:T(8,128)(2,1)} %constant.4.clone.table_far) | copy-start | bytes 7864324
